TPU v7x, 32 devices: a whole 2x2x4 slice. The times are simulated.
32 devices in a mesh: row: 8 (over z, y), col: 4 (over x, core).
Axes of the slice: x: 2, y: 2, z: 4, core: 2. Of those that a mesh axis runs over, the one named last changes fastest.
Arguments:
- eigvecs: float32 [131072, 1024], P('row', 'col'), may hold values from -6 to 6
- reflectors: float32 [4, 131072, 256], P(None, ('row', 'col'))
- factors: float32 [4, 256, 256], replicated, as said below
Outputs:
- transformed: float32 [131072, 1024], P('row', 'col')
Inputs may be any that keep to these rules, and one draw needn't show every extreme that they name: Each factors[k] is upper triangular with a positive diagonal.
All inputs are finite; a program needn't handle non-finite values.
Results may differ from a plain program's by a relative error of at most 0.00012.
Values sent between devices are 32-bit elements; how exact they have to be, the bound alone decides.
A program may use at most 192 MiB of HBM per device.

v0:
```python
import functools

import jax
import jax.numpy as jnp
from jax import lax
from jax.experimental import pallas as pl
from jax.experimental.pallas import tpu as pltpu
from jax.sharding import PartitionSpec as P

CORES = 2
MESH = pl.DeviceIdType.MESH
SCOPED = 26 * 1024 * 1024


def tile_of(rows, most):
    tile = most
    while rows % tile:
        tile //= 2
    return tile


def halves(value):
    high = value.astype(jnp.bfloat16)
    low = (value - high.astype(jnp.float32)).astype(jnp.bfloat16)
    return high, low


def three_pass(left, right, dims):
    left_high, left_low = left
    right_high, right_low = right
    dot = functools.partial(lax.dot_general, dimension_numbers=(dims, ((), ())), preferred_element_type=jnp.float32)
    return dot(left_high, right_high) + (dot(left_high, right_low) + dot(left_low, right_high))


def fused_kernel(
    size, height, chunk,
    eig_ref, refl_ref, fac_ref,
    field_ref, last_ref, coeffs_ref,
    other_ref, acc_ref, proj_ref, pieces_ref, high_ref, low_ref,
    field_sem, own_sem, mate_send, mate_recv, far_send, far_recv, pass_send, pass_recv,
    credit, scatter_send, scatter_recv, gather_send, gather_recv,
):
    me = lax.axis_index("col")
    row = lax.axis_index("row")
    mate = me + 1 - 2 * (me % 2)
    shifts = list(range(CORES, size, CORES))
    panels, rows, width = refl_ref.shape
    chunks = rows // chunk
    piece = width // height
    tile = tile_of(rows, 512)

    def slot(k):
        return last_ref if (panels - 1 - k) % 2 == 0 else other_ref

    def block(owner, start, count):
        return pl.ds(pl.multiple_of(owner * rows + start, count), count)

    def own_copy(k):
        return pltpu.make_async_copy(refl_ref.at[k], slot(k).at[block(me, 0, rows)], own_sem.at[k % 2])

    def mate_copy(k, owner):
        return pltpu.make_async_remote_copy(
            src_ref=refl_ref.at[k], dst_ref=slot(k).at[block(owner, 0, rows)],
            send_sem=mate_send.at[k % 2], recv_sem=mate_recv.at[k % 2],
            device_id={"col": mate}, device_id_type=MESH)

    def far_copy(k, i, c, owner):
        return pltpu.make_async_remote_copy(
            src_ref=refl_ref.at[k, pl.ds(pl.multiple_of(c * chunk, chunk), chunk)],
            dst_ref=slot(k).at[block(owner, c * chunk, chunk)],
            send_sem=far_send.at[k % 2, i, c], recv_sem=far_recv.at[k % 2, i, c],
            device_id={"col": (me + shifts[i]) % size}, device_id_type=MESH)

    def pass_copy(k, i, c, owner):
        view = slot(k).at[block(owner, c * chunk, chunk)]
        return pltpu.make_async_remote_copy(
            src_ref=view, dst_ref=view,
            send_sem=pass_send.at[k % 2, i, c], recv_sem=pass_recv.at[k % 2, i, c],
            device_id={"col": mate}, device_id_type=MESH)

    def send(k):
        def one(c, carry):
            for i in range(len(shifts)):
                far_copy(k, i, c, me).start()
            return carry

        lax.fori_loop(0, chunks, one, 0)
        own_copy(k).start()
        mate_copy(k, me).start()

    def sent(k):
        def one(c, carry):
            for i in range(len(shifts)):
                far_copy(k, i, c, me).wait_send()
                pass_copy(k, i, c, (me - shifts[i] + size) % size).wait_send()
            return carry

        lax.fori_loop(0, chunks, one, 0)
        mate_copy(k, me).wait_send()

    def inner(k, owner, start, count):
        view = block(owner, start, count)
        acc_ref[...] += three_pass(halves(slot(k)[view, :]), halves(field_ref[view, :]), ((0,), (0,)))

    def inner_block(k, owner):
        def one(t, carry):
            inner(k, owner, t * tile, tile)
            return carry

        lax.fori_loop(0, rows // tile, one, 0)

    def reduce_row():
        def scatter(d):
            peer = (row + d) % height
            return pltpu.make_async_remote_copy(
                src_ref=acc_ref.at[pl.ds(pl.multiple_of(peer * piece, piece), piece)], dst_ref=pieces_ref.at[d],
                send_sem=scatter_send.at[d], recv_sem=scatter_recv.at[d],
                device_id={"row": peer}, device_id_type=MESH)

        def gather(d, owner):
            view = proj_ref.at[pl.ds(pl.multiple_of(owner * piece, piece), piece)]
            return pltpu.make_async_remote_copy(
                src_ref=view, dst_ref=view,
                send_sem=gather_send.at[d], recv_sem=gather_recv.at[d],
                device_id={"row": (row + d) % height}, device_id_type=MESH)

        mine = pl.ds(pl.multiple_of(row * piece, piece), piece)
        for d in range(1, height):
            scatter(d).start()
        total = acc_ref[mine, :]
        for d in range(1, height):
            scatter(d).wait_recv()
            total = total + pieces_ref[d]
        proj_ref[mine, :] = total
        for d in range(1, height):
            gather(d, row).start()
        for d in range(1, height):
            gather(d, (row - d + height) % height).wait_recv()
        for d in range(1, height):
            scatter(d).wait_send()
            gather(d, row).wait_send()

    barrier = pltpu.get_barrier_semaphore()
    for d in range(1, height):
        pl.semaphore_signal(barrier, inc=1, device_id={"row": (row + d) % height}, device_id_type=MESH)
    for there in [mate] + [(me + shift) % size for shift in shifts]:
        pl.semaphore_signal(barrier, inc=1, device_id={"col": there}, device_id_type=MESH)
    pl.semaphore_wait(barrier, height - 1 + 1 + len(shifts))

    field_copy = pltpu.make_async_copy(eig_ref, field_ref, field_sem)
    send(0)
    field_copy.start()
    if panels > 1:
        send(1)
    field_copy.wait()

    for k in range(panels):
        acc_ref[...] = jnp.zeros_like(acc_ref)
        own_copy(k).wait()
        inner_block(k, me)
        mate_copy(k, mate).wait_recv()
        inner_block(k, mate)

        def far_step(c, carry):
            for i in range(len(shifts)):
                owner = (me - shifts[i] + size) % size
                far_copy(k, i, c, owner).wait_recv()
                pass_copy(k, i, c, owner).start()
                inner(k, owner, c * chunk, chunk)
            for i in range(len(shifts)):
                owner = (mate - shifts[i] + size) % size
                pass_copy(k, i, c, owner).wait_recv()
                inner(k, owner, c * chunk, chunk)
            return carry

        lax.fori_loop(0, chunks, far_step, 0)
        reduce_row()
        coeffs = jnp.dot(fac_ref[k], proj_ref[...], precision=lax.Precision.HIGHEST, preferred_element_type=jnp.float32)
        if k == panels - 1:
            coeffs_ref[...] = coeffs
            break
        high_ref[...], low_ref[...] = halves(coeffs)

        def update_step(t, carry):
            view = pl.ds(pl.multiple_of(t * tile, tile), tile)
            field_ref[view, :] -= three_pass(halves(slot(k)[view, :]), (high_ref[...], low_ref[...]), ((1,), (0,)))
            return carry

        lax.fori_loop(0, size * rows // tile, update_step, 0)
        if k + 2 < panels:
            sent(k)
            for i in range(len(shifts)):
                pl.semaphore_signal(credit.at[k, i], inc=1, device_id={"col": (me - shifts[i] + size) % size}, device_id_type=MESH)
            pl.semaphore_signal(credit.at[k, len(shifts)], inc=1, device_id={"col": mate}, device_id_type=MESH)
            for i in range(len(shifts) + 1):
                pl.semaphore_wait(credit.at[k, i], 1)
            send(k + 2)
    for k in range(max(panels - 2, 0), panels):
        sent(k)


def fused(size, height, eigvecs, reflectors, factors):
    panels, rows, width = reflectors.shape
    total, columns = eigvecs.shape
    chunk = max(min(rows, 64), rows // 16)
    chunks = rows // chunk
    far = max(size // CORES - 1, 1)
    dma = pltpu.SemaphoreType.DMA
    return pl.pallas_call(
        functools.partial(fused_kernel, size, height, chunk),
        out_shape=[
            pltpu.VMEM((total, columns), jnp.float32),
            pltpu.VMEM((total, width), jnp.float32),
            pltpu.VMEM((width, columns), jnp.float32),
        ],
        in_specs=[pl.BlockSpec(memory_space=pl.ANY)] * 2 + [pl.BlockSpec(memory_space=pltpu.VMEM)],
        out_specs=[pl.BlockSpec(memory_space=pltpu.VMEM)] * 3,
        scratch_shapes=[
            pltpu.VMEM((total, width), jnp.float32),
            pltpu.VMEM((width, columns), jnp.float32),
            pltpu.VMEM((width, columns), jnp.float32),
            pltpu.VMEM((height, width // height, columns), jnp.float32),
            pltpu.VMEM((width, columns), jnp.bfloat16),
            pltpu.VMEM((width, columns), jnp.bfloat16),
            dma, dma((2,)), dma((2,)), dma((2,)),
            dma((2, far, chunks)), dma((2, far, chunks)), dma((2, far, chunks)), dma((2, far, chunks)),
            pltpu.SemaphoreType.REGULAR((max(panels, 1), far + 1)),
            dma((height,)), dma((height,)), dma((height,)), dma((height,)),
        ],
        compiler_params=pltpu.CompilerParams(collective_id=0, has_side_effects=True, vmem_limit_bytes=SCOPED),
        name="fused",
    )(*[pltpu.with_memory_space_constraint(value, pltpu.HBM) for value in (eigvecs, reflectors, factors)])


DEPTH = 4


def final_kernel(field_ref, vectors_ref, coeffs_ref, out_ref, high_ref, low_ref, stage_ref, sem):
    tile = stage_ref.shape[1]
    steps = field_ref.shape[0] // tile
    high_ref[...], low_ref[...] = halves(coeffs_ref[...])

    def store(t):
        view = pl.ds(pl.multiple_of(t * tile, tile), tile)
        return pltpu.make_async_copy(stage_ref.at[t % DEPTH], out_ref.at[view], sem.at[t % DEPTH])

    def step(t, carry):
        view = pl.ds(pl.multiple_of(t * tile, tile), tile)

        @pl.when(t >= DEPTH)
        def _():
            store(t - DEPTH).wait()

        stage_ref[t % DEPTH] = field_ref[view, :] - three_pass(halves(vectors_ref[view, :]), (high_ref[...], low_ref[...]), ((1,), (0,)))
        store(t).start()
        return carry

    lax.fori_loop(0, steps, step, 0)
    for t in range(max(steps - DEPTH, 0), steps):
        store(t).wait()


def final(field, vectors, coeffs):
    total, columns = field.shape
    width = vectors.shape[1]
    tile = tile_of(total, 512)
    return pl.pallas_call(
        final_kernel,
        out_shape=jax.ShapeDtypeStruct(field.shape, jnp.float32),
        in_specs=[pl.BlockSpec(memory_space=pltpu.VMEM)] * 3,
        out_specs=pl.BlockSpec(memory_space=pl.ANY),
        scratch_shapes=[
            pltpu.VMEM((width, columns), jnp.bfloat16),
            pltpu.VMEM((width, columns), jnp.bfloat16),
            pltpu.VMEM((DEPTH, tile, columns), jnp.float32),
            pltpu.SemaphoreType.DMA((DEPTH,)),
        ],
        compiler_params=pltpu.CompilerParams(vmem_limit_bytes=SCOPED),
        name="final",
    )(*[pltpu.with_memory_space_constraint(value, pltpu.VMEM) for value in (field, vectors, coeffs)])


def body(size, height, eigvecs, reflectors, factors):
    return final(*fused(size, height, eigvecs, reflectors, factors))


def solution(mesh):
    in_specs = (P("row", "col"), P(None, ("row", "col"), None), P())
    out_specs = P("row", "col")
    return jax.shard_map(functools.partial(body, mesh.shape["col"], mesh.shape["row"]), mesh=mesh, in_specs=in_specs, out_specs=out_specs, check_vma=False)
```

profile of v0, /device:TPU:0, one launch (start us, length us, event | category | flops | bytes accessed | tf_op | source)
XLA Modules:
  0.0 397.3 jit_solution(10092968999541579927)
XLA Ops:
  0.0 384.2 %fused.1 = (f32[16384,256]{1,0:T(8,128)S(1)}, f32[16384,256]{1,0:T(8,128)S(1)}, f32[256,256]{1,0:T(8,128)S(1)}) custom-call(f32[16384,256]{1,0:T(8,128)} %eig_ref.1, f32[4,4096,256]{2,1,0:T(8,128)} %refl_ref.1, f32[4,256,256]{2,1,0:T(8,128)} %fac_ref.1), custom_call_target="tpu_custom_call" | custom-call | tf_op jit(solution)/shard_map/fused/pallas_call | solution.py:209
  384.2 13.0 %final.1 = f32[16384,256]{1,0:T(8,128)} custom-call(f32[16384,256]{1,0:T(8,128)S(1)} %get-tuple-element.8.field_ref, f32[16384,256]{1,0:T(8,128)S(1)} %get-tuple-element.9.vectors_ref, f32[256,256]{1,0:T(8,128)S(1)} %get-tuple-element.10.coeffs_ref), custom_call_target="tpu_custom_call" | custom-call | tf_op jit(solution)/shard_map/final/pallas_call | solution.py:267
where the time goes:
time: 398 us; the launch traced here: 397 us
  Pallas kernels  397 us (100%)
    pallas_call x1, Pallas kernels, fused(): pl.pallas_call(functools.partial(fused_kernel, size, height, chunk), out_...  384 us
    pallas_call x1, Pallas kernels, final(): pl.pallas_call(final_kernel, out_shape=jax.ShapeDtypeStruct(field.shape,...  13 us

commit v1 on v0

v1 whole, which is shorter than its diff:
```python
import functools

import jax
import jax.numpy as jnp
from jax import lax
from jax.experimental import pallas as pl
from jax.experimental.pallas import tpu as pltpu
from jax.sharding import PartitionSpec as P

CORES = 2
MESH = pl.DeviceIdType.MESH
SCOPED = 26 * 1024 * 1024


def tile_of(rows, most):
    tile = most
    while rows % tile:
        tile //= 2
    return tile


def halves(value):
    high = value.astype(jnp.bfloat16)
    low = (value - high.astype(jnp.float32)).astype(jnp.bfloat16)
    return high, low


def three_pass(left, right, dims):
    left_high, left_low = left
    right_high, right_low = right
    left_dim, right_dim = dims
    left_all = jnp.concatenate([left_high, left_high, left_low], left_dim)
    right_all = jnp.concatenate([right_high, right_low, right_high], right_dim)
    return lax.dot_general(left_all, right_all, (((left_dim,), (right_dim,)), ((), ())), preferred_element_type=jnp.float32)


def whole_product(left, right):
    return jnp.dot(left, right, precision=lax.Precision.HIGHEST, preferred_element_type=jnp.float32)


def spans_of(width, height):
    half = width // 2
    return [(half, half), (0, half)] if half % 128 == 0 and half % (8 * height) == 0 else [(0, width)]


def fused_kernel(
    size, height, chunk,
    eig_ref, refl_ref, fac_ref,
    field_ref, last_ref, coeffs_ref,
    other_ref, acc_ref, proj_ref, pieces_ref, high_ref, low_ref, square_ref, rest_ref,
    field_sem, square_sem, token, own_sem, mate_send, mate_recv, far_send, far_recv, pass_send, pass_recv,
    credit, scatter_send, scatter_recv, gather_send, gather_recv,
):
    me = lax.axis_index("col")
    row = lax.axis_index("row")
    mate = me + 1 - 2 * (me % 2)
    shifts = list(range(CORES, size, CORES))
    panels, rows, width = refl_ref.shape
    chunks = rows // chunk
    tile = tile_of(rows, 1024)
    whole = (0, width)
    spans = spans_of(width, height)

    def slot(k):
        return last_ref if (panels - 1 - k) % 2 == 0 else other_ref

    def block(owner, start, count):
        return pl.ds(pl.multiple_of(owner * rows + start, count), count)

    def own_copy(k):
        return pltpu.make_async_copy(refl_ref.at[k], slot(k).at[block(me, 0, rows)], own_sem.at[k % 2])

    def mate_copy(k, owner):
        return pltpu.make_async_remote_copy(
            src_ref=refl_ref.at[k], dst_ref=slot(k).at[block(owner, 0, rows)],
            send_sem=mate_send.at[k % 2], recv_sem=mate_recv.at[k % 2],
            device_id={"col": mate}, device_id_type=MESH)

    def parts_of(k):
        if k < panels - 1 or len(spans) == 1:
            return [(k % 2, whole)]
        return [(k % 2, spans[0]), (2, spans[1])]

    def far_copy(k, part, i, c, owner):
        plane, (left, count) = part
        return pltpu.make_async_remote_copy(
            src_ref=refl_ref.at[k, pl.ds(pl.multiple_of(c * chunk, chunk), chunk), pl.ds(left, count)],
            dst_ref=slot(k).at[block(owner, c * chunk, chunk), pl.ds(left, count)],
            send_sem=far_send.at[plane, i, c], recv_sem=far_recv.at[plane, i, c],
            device_id={"col": (me + shifts[i]) % size}, device_id_type=MESH)

    def pass_copy(k, part, i, c, owner):
        plane, (left, count) = part
        view = slot(k).at[block(owner, c * chunk, chunk), pl.ds(left, count)]
        return pltpu.make_async_remote_copy(
            src_ref=view, dst_ref=view,
            send_sem=pass_send.at[plane, i, c], recv_sem=pass_recv.at[plane, i, c],
            device_id={"col": mate}, device_id_type=MESH)

    def send(k):
        for part in parts_of(k):
            def one(c, carry):
                for i in range(len(shifts)):
                    far_copy(k, part, i, c, me).start()
                return carry

            lax.fori_loop(0, chunks, one, 0)
        own_copy(k).start()
        mate_copy(k, me).start()

    def sent(k):
        for part in parts_of(k):
            def one(c, carry):
                for i in range(len(shifts)):
                    far_copy(k, part, i, c, me).wait_send()
                    pass_copy(k, part, i, c, (me - shifts[i] + size) % size).wait_send()
                return carry

            lax.fori_loop(0, chunks, one, 0)
        mate_copy(k, me).wait_send()

    def inner(k, span, owner, start, count):
        view = block(owner, start, count)
        left, many = span
        some = pl.ds(left, many)
        acc_ref[some, :] += three_pass(halves(slot(k)[view, some]), halves(field_ref[view, :]), (0, 0))

    def inner_block(k, owner):
        def one(t, carry):
            inner(k, whole, owner, t * tile, tile)
            return carry

        lax.fori_loop(0, rows // tile, one, 0)

    def far_chunk(k, part, c):
        for i in range(len(shifts)):
            owner = (me - shifts[i] + size) % size
            far_copy(k, part, i, c, owner).wait_recv()
            pass_copy(k, part, i, c, owner).start()
            inner(k, part[1], owner, c * chunk, chunk)
        for i in range(len(shifts)):
            owner = (mate - shifts[i] + size) % size
            pass_copy(k, part, i, c, owner).wait_recv()
            inner(k, part[1], owner, c * chunk, chunk)

    def update(k, span, view):
        some = pl.ds(*span)
        field_ref[view, :] -= three_pass(halves(slot(k)[view, some]), (high_ref[some, :], low_ref[some, :]), (1, 0))

    def reduce_row(span, between):
        first, many = span
        piece = many // height
        part = pl.ds(0, piece)

        def scatter(d):
            peer = (row + d) % height
            return pltpu.make_async_remote_copy(
                src_ref=acc_ref.at[pl.ds(pl.multiple_of(first + peer * piece, piece), piece)], dst_ref=pieces_ref.at[d, part],
                send_sem=scatter_send.at[d], recv_sem=scatter_recv.at[d],
                device_id={"row": peer}, device_id_type=MESH)

        def gather(d, owner):
            view = proj_ref.at[pl.ds(pl.multiple_of(first + owner * piece, piece), piece)]
            return pltpu.make_async_remote_copy(
                src_ref=view, dst_ref=view,
                send_sem=gather_send.at[d], recv_sem=gather_recv.at[d],
                device_id={"row": (row + d) % height}, device_id_type=MESH)

        mine = pl.ds(pl.multiple_of(first + row * piece, piece), piece)
        for d in range(1, height):
            scatter(d).start()
        between()
        total = acc_ref[mine, :]
        for d in range(1, height):
            scatter(d).wait_recv()
            total = total + pieces_ref[d, part, :]
        proj_ref[mine, :] = total
        for d in range(1, height):
            gather(d, row).start()
        for d in range(1, height):
            gather(d, (row - d + height) % height).wait_recv()
        for d in range(1, height):
            scatter(d).wait_send()
            gather(d, row).wait_send()

    barrier = pltpu.get_barrier_semaphore()
    for there in [mate] + [(me + shift) % size for shift in shifts]:
        pl.semaphore_signal(barrier, inc=1, device_id={"col": there}, device_id_type=MESH)
    lowest, highest = row == 0, row == height - 1
    below, above = jnp.maximum(row - 1, 0), jnp.minimum(row + 1, height - 1)

    @pl.when(jnp.logical_not(lowest))
    def _():
        pl.semaphore_signal(barrier, inc=1, device_id={"row": below}, device_id_type=MESH)

    @pl.when(jnp.logical_not(highest))
    def _():
        pl.semaphore_signal(barrier, inc=1, device_id={"row": above}, device_id_type=MESH)

    pl.semaphore_wait(barrier, 1 + len(shifts) + jnp.where(lowest, 0, 1) + jnp.where(highest, 0, 1))

    def greet_row():
        @pl.when(jnp.logical_not(lowest))
        def _():
            pl.semaphore_wait(token.at[0], 1)

        @pl.when(jnp.logical_not(highest))
        def _():
            pl.semaphore_signal(token.at[0], inc=1, device_id={"row": above}, device_id_type=MESH)
            pl.semaphore_wait(token.at[1], 1)

        @pl.when(jnp.logical_not(lowest))
        def _():
            pl.semaphore_signal(token.at[1], inc=1, device_id={"row": below}, device_id_type=MESH)

    field_copy = pltpu.make_async_copy(eig_ref, field_ref, field_sem)
    square_copy = pltpu.make_async_copy(fac_ref, square_ref, square_sem)
    send(0)
    field_copy.start()
    square_copy.start()
    if panels > 1:
        send(1)
    field_copy.wait()
    square_copy.wait()
    greet_row()

    def nothing():
        pass

    def finish():
        for k in range(max(panels - 2, 0), panels):
            sent(k)

    for k in range(panels):
        acc_ref[...] = jnp.zeros_like(acc_ref)
        own_copy(k).wait()
        inner_block(k, me)
        mate_copy(k, mate).wait_recv()
        inner_block(k, mate)
        first_part = parts_of(k)[0]

        def far_step(c, carry):
            far_chunk(k, first_part, c)
            return carry

        lax.fori_loop(0, chunks, far_step, 0)
        reduce_row(first_part[1], nothing)
        if k == panels - 1:
            break
        high_ref[...], low_ref[...] = halves(whole_product(square_ref[k], proj_ref[...]))

        def update_step(t, carry):
            update(k, whole, pl.ds(pl.multiple_of(t * tile, tile), tile))
            return carry

        lax.fori_loop(0, size * rows // tile, update_step, 0)
        if k + 2 < panels:
            sent(k)
            for i in range(len(shifts)):
                pl.semaphore_signal(credit.at[k, i], inc=1, device_id={"col": (me - shifts[i] + size) % size}, device_id_type=MESH)
            pl.semaphore_signal(credit.at[k, len(shifts)], inc=1, device_id={"col": mate}, device_id_type=MESH)
            for i in range(len(shifts) + 1):
                pl.semaphore_wait(credit.at[k, i], 1)
            send(k + 2)

    k = panels - 1
    if len(spans) == 1:
        finish()
        coeffs_ref[...] = whole_product(square_ref[k], proj_ref[...])
    else:
        (later, many), (_, few) = spans
        below, above = pl.ds(later, many), pl.ds(0, few)
        high_ref[below, :], low_ref[below, :] = halves(whole_product(square_ref[k, below, below], proj_ref[below, :]))
        rest_ref[...] = whole_product(square_ref[k, above, below], proj_ref[below, :])
        last_part = parts_of(k)[1]

        def update_far(c):
            for shift in shifts:
                for origin in (me, mate):
                    update(k, spans[0], block((origin - shift + size) % size, c * chunk, chunk))

        def last_step(c, carry):
            for origin in (me, mate):
                update(k, spans[0], block(origin, c * chunk, chunk))

            @pl.when(c > 0)
            def _():
                update_far(c - 1)

            far_chunk(k, last_part, c)
            return carry

        lax.fori_loop(0, chunks, last_step, 0)

        def meanwhile():
            update_far(chunks - 1)
            finish()

        reduce_row(spans[1], meanwhile)
        coeffs_ref[...] = rest_ref[...] + whole_product(square_ref[k, above, above], proj_ref[above, :])


def fused(size, height, eigvecs, reflectors, factors):
    panels, rows, width = reflectors.shape
    total, columns = eigvecs.shape
    chunk = max(min(rows, 64), rows // 16)
    chunks = rows // chunk
    kept = spans_of(width, height)[-1][1]
    far = max(size // CORES - 1, 1)
    dma = pltpu.SemaphoreType.DMA
    return pl.pallas_call(
        functools.partial(fused_kernel, size, height, chunk),
        out_shape=[
            pltpu.VMEM((total, columns), jnp.float32),
            pltpu.VMEM((total, width), jnp.float32),
            pltpu.VMEM((kept, columns), jnp.float32),
        ],
        in_specs=[pl.BlockSpec(memory_space=pl.ANY)] * 3,
        out_specs=[pl.BlockSpec(memory_space=pltpu.VMEM)] * 3,
        scratch_shapes=[
            pltpu.VMEM((total, width), jnp.float32),
            pltpu.VMEM((width, columns), jnp.float32),
            pltpu.VMEM((width, columns), jnp.float32),
            pltpu.VMEM((height, width // height, columns), jnp.float32),
            pltpu.VMEM((width, columns), jnp.bfloat16),
            pltpu.VMEM((width, columns), jnp.bfloat16),
            pltpu.VMEM((panels, width, width), jnp.float32),
            pltpu.VMEM((kept, columns), jnp.float32),
            dma, dma, pltpu.SemaphoreType.REGULAR((2,)), dma((2,)), dma((2,)), dma((2,)),
            dma((3, far, chunks)), dma((3, far, chunks)), dma((3, far, chunks)), dma((3, far, chunks)),
            pltpu.SemaphoreType.REGULAR((max(panels, 1), far + 1)),
            dma((height,)), dma((height,)), dma((height,)), dma((height,)),
        ],
        compiler_params=pltpu.CompilerParams(collective_id=0, has_side_effects=True, vmem_limit_bytes=SCOPED),
        name="fused",
    )(*[pltpu.with_memory_space_constraint(value, pltpu.HBM) for value in (eigvecs, reflectors, factors)])


DEPTH = 4


def final_kernel(field_ref, vectors_ref, coeffs_ref, out_ref, high_ref, low_ref, stage_ref, sem):
    tile = stage_ref.shape[1]
    steps = field_ref.shape[0] // tile
    kept = pl.ds(0, coeffs_ref.shape[0])
    high_ref[...], low_ref[...] = halves(coeffs_ref[...])

    def store(t):
        view = pl.ds(pl.multiple_of(t * tile, tile), tile)
        return pltpu.make_async_copy(stage_ref.at[t % DEPTH], out_ref.at[view], sem.at[t % DEPTH])

    def step(t, carry):
        view = pl.ds(pl.multiple_of(t * tile, tile), tile)

        @pl.when(t >= DEPTH)
        def _():
            store(t - DEPTH).wait()

        stage_ref[t % DEPTH] = field_ref[view, :] - three_pass(halves(vectors_ref[view, kept]), (high_ref[...], low_ref[...]), (1, 0))
        store(t).start()
        return carry

    lax.fori_loop(0, steps, step, 0)
    for t in range(max(steps - DEPTH, 0), steps):
        store(t).wait()


def final(field, vectors, coeffs):
    total, columns = field.shape
    width = coeffs.shape[0]
    tile = tile_of(total, 2048)
    return pl.pallas_call(
        final_kernel,
        out_shape=jax.ShapeDtypeStruct(field.shape, jnp.float32),
        in_specs=[pl.BlockSpec(memory_space=pltpu.VMEM)] * 3,
        out_specs=pl.BlockSpec(memory_space=pl.ANY),
        scratch_shapes=[
            pltpu.VMEM((width, columns), jnp.bfloat16),
            pltpu.VMEM((width, columns), jnp.bfloat16),
            pltpu.VMEM((DEPTH, tile, columns), jnp.float32),
            pltpu.SemaphoreType.DMA((DEPTH,)),
        ],
        compiler_params=pltpu.CompilerParams(vmem_limit_bytes=SCOPED),
        name="final",
    )(*[pltpu.with_memory_space_constraint(value, pltpu.VMEM) for value in (field, vectors, coeffs)])


def body(size, height, eigvecs, reflectors, factors):
    return final(*fused(size, height, eigvecs, reflectors, factors))


def solution(mesh):
    in_specs = (P("row", "col"), P(None, ("row", "col"), None), P())
    out_specs = P("row", "col")
    return jax.shard_map(functools.partial(body, mesh.shape["col"], mesh.shape["row"]), mesh=mesh, in_specs=in_specs, out_specs=out_specs, check_vma=False)
```

time: 398 us -> 390 us (0.980)
  Pallas kernels: 397 us -> 390 us
    pallas_call x1, Pallas kernels: 13 us -> 7.02 us  [final(): pl.pallas_call(final_kernel, out_shape=jax.ShapeDtypeStruct(field.shape,...]
where the time goes in v1:
time: 390 us
  Pallas kernels  390 us (100%)
    pallas_call x1, Pallas kernels, fused(): pl.pallas_call(functools.partial(fused_kernel, size, height, chunk), out_...  383 us

profile of v1, /device:TPU:0, one launch (start us, length us, event | category | flops | bytes accessed | tf_op | source)
XLA Modules:
  0.0 390.3 jit_solution(3701067025472732228)
XLA Ops:
  0.0 383.2 %fused.1 = (f32[16384,256]{1,0:T(8,128)S(1)}, f32[16384,256]{1,0:T(8,128)S(1)}, f32[128,256]{1,0:T(8,128)S(1)}) custom-call(f32[16384,256]{1,0:T(8,128)} %eig_ref.1, f32[4,4096,256]{2,1,0:T(8,128)} %refl_ref.1, f32[4,256,256]{2,1,0:T(8,128)} %fac_ref.1), custom_call_target="tpu_custom_call" | custom-call | tf_op jit(solution)/shard_map/fused/pallas_call | solution.py:311
  383.2 7.0 %final.1 = f32[16384,256]{1,0:T(8,128)} custom-call(f32[16384,256]{1,0:T(8,128)S(1)} %get-tuple-element.8.field_ref, f32[16384,256]{1,0:T(8,128)S(1)} %get-tuple-element.9.vectors_ref, f32[128,256]{1,0:T(8,128)S(1)} %get-tuple-element.10.coeffs_ref), custom_call_target="tpu_custom_call" | custom-call | tf_op jit(solution)/shard_map/final/pallas_call | solution.py:372

commit v2 on v1

--- a/solution.py
+++ b/solution.py
@@ -132,12 +132,14 @@
 
         lax.fori_loop(0, rows // tile, one, 0)
 
-    def far_chunk(k, part, c):
+    def near_chunk(k, part, c):
         for i in range(len(shifts)):
             owner = (me - shifts[i] + size) % size
             far_copy(k, part, i, c, owner).wait_recv()
             pass_copy(k, part, i, c, owner).start()
             inner(k, part[1], owner, c * chunk, chunk)
+
+    def passed_chunk(k, part, c):
         for i in range(len(shifts)):
             owner = (mate - shifts[i] + size) % size
             pass_copy(k, part, i, c, owner).wait_recv()
@@ -240,10 +242,16 @@
         first_part = parts_of(k)[0]
 
         def far_step(c, carry):
-            far_chunk(k, first_part, c)
+            near_chunk(k, first_part, c)
+
+            @pl.when(c > 0)
+            def _():
+                passed_chunk(k, first_part, c - 1)
+
             return carry
 
         lax.fori_loop(0, chunks, far_step, 0)
+        passed_chunk(k, first_part, chunks - 1)
         reduce_row(first_part[1], nothing)
         if k == panels - 1:
             break
@@ -283,17 +291,24 @@
             for origin in (me, mate):
                 update(k, spans[0], block(origin, c * chunk, chunk))
 
+            @pl.when(c > 1)
+            def _():
+                update_far(c - 2)
+
+            near_chunk(k, last_part, c)
+
             @pl.when(c > 0)
             def _():
-                update_far(c - 1)
-
-            far_chunk(k, last_part, c)
+                passed_chunk(k, last_part, c - 1)
+
             return carry
 
         lax.fori_loop(0, chunks, last_step, 0)
+        passed_chunk(k, last_part, chunks - 1)
 
         def meanwhile():
-            update_far(chunks - 1)
+            for c in range(max(chunks - 2, 0), chunks):
+                update_far(c)
             finish()
 
         reduce_row(spans[1], meanwhile)

time: 390 us -> 387 us (level)
  no operation moved by 1% of the time
where the time goes in v2:
time: 387 us
  Pallas kernels  387 us (100%)
    pallas_call x1, Pallas kernels, fused(): pl.pallas_call(functools.partial(fused_kernel, size, height, chunk), out_...  380 us

profile of v2, /device:TPU:0, one launch (start us, length us, event | category | flops | bytes accessed | tf_op | source)
XLA Modules:
  0.0 386.8 jit_solution(4969032845989689522)
XLA Ops:
  0.0 379.7 %fused.1 = (f32[16384,256]{1,0:T(8,128)S(1)}, f32[16384,256]{1,0:T(8,128)S(1)}, f32[128,256]{1,0:T(8,128)S(1)}) custom-call(f32[16384,256]{1,0:T(8,128)} %eig_ref.1, f32[4,4096,256]{2,1,0:T(8,128)} %refl_ref.1, f32[4,256,256]{2,1,0:T(8,128)} %fac_ref.1), custom_call_target="tpu_custom_call" | custom-call | tf_op jit(solution)/shard_map/fused/pallas_call | solution.py:326
  379.8 7.0 %final.1 = f32[16384,256]{1,0:T(8,128)} custom-call(f32[16384,256]{1,0:T(8,128)S(1)} %get-tuple-element.8.field_ref, f32[16384,256]{1,0:T(8,128)S(1)} %get-tuple-element.9.vectors_ref, f32[128,256]{1,0:T(8,128)S(1)} %get-tuple-element.10.coeffs_ref), custom_call_target="tpu_custom_call" | custom-call | tf_op jit(solution)/shard_map/final/pallas_call | solution.py:387
